TPU v7x, 256 devices: a whole 4x4x8 slice. The times are simulated.
256 devices in a mesh: seq: 16 (over z, core), head: 16 (over x, y).
Axes of the slice: x: 4, y: 4, z: 8, core: 2. Of those that a mesh axis runs over, the one named last changes fastest.
Arguments:
- grad_output: bfloat16 [16384, 4096], P('seq', 'head'), may hold values from -6 to 6
- out_weight: bfloat16 [4096, 8192], P('seq', 'head'), may hold values from -0.0625 to 0.0625
- ssd_out: bfloat16 [16384, 8192], P('seq', 'head'), may hold values from -520 to 520
- gate: bfloat16 [16384, 8192], P('seq', 'head'), may hold values from -5 to 5
- norm_weight: float32 [8192], P('head'), may hold values from 0.5 to 1.5
- time_step: float32 [128, 16384], P('head', 'seq'), may hold values from 0.01 to 0.1
- log_decay: float32 [128, 16384], P('head', 'seq'), may hold values from -0.7 to 0
- state_in: bfloat16 [16384, 8, 128], P('seq'), may hold values from -1.796875 to 1.796875
- state_out: bfloat16 [16384, 8, 128], P('seq'), may hold values from -1.796875 to 1.796875
- skip: float32 [128], P('head'), may hold values from 0.5 to 1.5
Outputs:
- grad_x: bfloat16 [16384, 8192], P('seq', 'head')
- grad_gate: bfloat16 [16384, 8192], P('seq', 'head')
- grad_out_weight: float32 [4096, 8192], P('seq', 'head')
All inputs are finite; a program needn't handle non-finite values.
Results may differ from a plain program's by a relative error of at most 0.014.
Values may be sent and summed in bfloat16 or wider, within the bound.
A program may use at most 128 MiB of HBM per device.

v0:
```python
import math
import jax
import jax.numpy as jnp
from jax import lax
from jax.sharding import Mesh
from jax.sharding import PartitionSpec as P

HEADS = 128
GROUPS = 8
BLOCK_LEN = 256
HEAD = ("head_0", "head_1")
SEQ = ("seq_0", "seq_1")
epsilon = 1e-05


def over_axes(x, axes):
    for axis in axes:
        x = lax.psum(x, axis)
    return x


def nothing_yet(x, identity):
    return jax.tree.map(
        lambda part, zero: jnp.zeros_like(part) + jnp.asarray(zero, part.dtype), x, identity
    )


def carried_in(x, axes, combine, identity):
    before = start = nothing_yet(x, identity)
    running = x
    for axis in reversed(axes):
        size, here = (lax.axis_size(axis), lax.axis_index(axis))
        pieces = jax.tree.map(lambda part: lax.all_gather(part, axis), running)
        inside, running = (start, start)
        for k in reversed(range(size)):
            passed = k > here
            running = combine(running, jax.tree.map(lambda part: part[k], pieces))
            inside = jax.tree.map(lambda new, old: jnp.where(passed, new, old), running, inside)
        before = combine(inside, before)
    return before


def on_device(
    grad_output,
    out_weight,
    ssd_out,
    gate,
    norm_weight,
    time_step,
    log_decay,
    state_in,
    state_out,
    skip,
):
    tok_rows = ssd_out.shape[0]
    local_width = ssd_out.shape[1]
    total_width = local_width * lax.axis_size(HEAD)
    full_grad = lax.all_gather(grad_output, HEAD, axis=1, tiled=True)
    values = ssd_out.astype(jnp.float32)
    gate_values = gate.astype(jnp.float32)
    sigmoid_gate = jax.nn.sigmoid(gate_values)
    silu_gate = gate_values * sigmoid_gate
    gated_values = values * silu_gate
    local_squares = jnp.sum(gated_values * gated_values, axis=1)
    columns = full_grad
    normed_grad = jnp.dot(
        columns,
        lax.all_gather(out_weight, SEQ, axis=0, tiled=True),
        preferred_element_type=jnp.float32,
    )
    squares = over_axes(local_squares, HEAD)
    weighted = over_axes(jnp.sum(norm_weight * normed_grad * gated_values, axis=1), HEAD)
    inverse_rms = lax.rsqrt(squares[:, None] / total_width + epsilon)
    normed = (gated_values * inverse_rms * norm_weight).astype(jnp.bfloat16)
    gated_grad = (
        inverse_rms * norm_weight * normed_grad
        - gated_values * inverse_rms**3 * weighted[:, None] / total_width
    )
    grad_gate = (
        gated_grad * values * sigmoid_gate * (1.0 + gate_values * (1.0 - sigmoid_gate))
    ).astype(jnp.bfloat16)
    grad_ssd = (gated_grad * silu_gate).astype(jnp.bfloat16)
    columns = full_grad
    weight_sum = lax.psum_scatter(
        lax.dot_general(
            columns, normed, (((0,), (0,)), ((), ())), preferred_element_type=jnp.float32
        ).astype(jnp.bfloat16),
        SEQ,
        scatter_dimension=0,
        tiled=True,
    ).astype(jnp.float32)
    grad_out_weight = weight_sum * (1.0 / math.sqrt(tok_rows * lax.axis_size(SEQ)))
    heads_here = time_step.shape[0]
    head_width = local_width // heads_here
    blocks = tok_rows // BLOCK_LEN
    state_width = state_in.shape[2]
    group_count = state_in.shape[1]
    first_head = lax.axis_index(HEAD) * heads_here
    head_ids = first_head + jnp.arange(heads_here, dtype=jnp.int32)
    group_ids = head_ids // (HEADS // GROUPS)
    group_pick = (group_ids[:, None] == jnp.arange(group_count, dtype=jnp.int32)[None, :]).astype(
        jnp.bfloat16
    )
    b_heads = jnp.einsum(
        "tgn,hg->htn", state_in, group_pick, preferred_element_type=jnp.float32
    ).astype(jnp.bfloat16)
    b_heads = b_heads.reshape(heads_here, blocks, BLOCK_LEN, state_width)
    c_heads = jnp.einsum(
        "tgn,hg->htn", state_out, group_pick, preferred_element_type=jnp.float32
    ).astype(jnp.bfloat16)
    c_heads = c_heads.reshape(heads_here, blocks, BLOCK_LEN, state_width)
    grad_heads = grad_ssd.reshape(tok_rows, heads_here, head_width).transpose(1, 0, 2)
    grad_heads = grad_heads.reshape(heads_here, blocks, BLOCK_LEN, head_width)
    cumulative = jnp.cumsum(log_decay.reshape(heads_here, blocks, BLOCK_LEN), axis=2)
    block_total = cumulative[..., -1]
    sequence_indices = jnp.arange(BLOCK_LEN)
    upper_mask = sequence_indices[None, :] >= sequence_indices[:, None]
    scores = jnp.einsum("hktn,hksn->hkts", b_heads, c_heads, preferred_element_type=jnp.float32)
    log_gap = cumulative[..., None, :] - cumulative[..., :, None]
    block_weights = jnp.where(upper_mask, scores * jnp.exp(jnp.minimum(log_gap, 0.0)), 0.0).astype(
        jnp.bfloat16
    )
    within = jnp.einsum(
        "hkts,hksp->hktp", block_weights, grad_heads, preferred_element_type=jnp.float32
    )
    grad_float = grad_heads.astype(jnp.float32)
    scaled = (jnp.exp(cumulative)[..., None] * grad_float).astype(jnp.bfloat16)
    block_state = jnp.einsum("hksp,hksn->hkpn", scaled, c_heads, preferred_element_type=jnp.float32)

    def fold_block(carried, inputs):
        state_now, total_now = inputs
        return (state_now + jnp.exp(total_now)[:, None, None] * carried, carried)

    zero_state = jnp.zeros((heads_here, head_width, state_width), jnp.float32)
    summary, inside = lax.scan(
        fold_block, zero_state, (block_state.transpose(1, 0, 2, 3), block_total.T), reverse=True
    )
    decay_total = jnp.exp(jnp.sum(block_total, axis=1))
    tail_decay = jnp.exp(
        jnp.sum(block_total, axis=1, keepdims=True) - jnp.cumsum(block_total, axis=1)
    )

    def combine_pair(earlier, later):
        return (later[0] * earlier[0], later[1] + later[0][:, None, None] * earlier[1])

    identity = (jnp.ones((heads_here,), jnp.float32), zero_state)
    prefix = carried_in((decay_total, summary), SEQ, combine_pair, identity)
    remote = prefix[1]
    full_states = inside.transpose(1, 0, 2, 3) + tail_decay[..., None, None] * remote[:, None]
    carry_low = full_states.astype(jnp.bfloat16)
    across = jnp.einsum("hkpn,hktn->hktp", carry_low, b_heads, preferred_element_type=jnp.float32)
    across = across * jnp.exp(block_total[..., None] - cumulative)[..., None]
    step_sizes = time_step.reshape(heads_here, blocks, BLOCK_LEN)
    grad_head = step_sizes[..., None] * (within + across) + skip[:, None, None, None] * grad_float
    grad_x = (
        grad_head.reshape(heads_here, tok_rows, head_width)
        .transpose(1, 0, 2)
        .reshape(tok_rows, local_width)
    )
    return (grad_x.astype(jnp.bfloat16), grad_gate, grad_out_weight)


def solution(mesh):
    finer = Mesh(mesh.devices.reshape(8, 2, 4, 4), ("seq_0", "seq_1", "head_0", "head_1"))
    return jax.shard_map(
        on_device,
        mesh=finer,
        in_specs=(
            P(SEQ, HEAD),
            P(SEQ, HEAD),
            P(SEQ, HEAD),
            P(SEQ, HEAD),
            P(HEAD),
            P(HEAD, SEQ),
            P(HEAD, SEQ),
            P(SEQ, None, None),
            P(SEQ, None, None),
            P(HEAD),
        ),
        out_specs=(P(SEQ, HEAD), P(SEQ, HEAD), P(SEQ, HEAD)),
        check_vma=False,
    )
```

profile of v0, /device:TPU:2, one launch (start us, length us, event | category | flops | bytes accessed | tf_op | source)
XLA Modules:
  0.0 294.2 jit_solution(11251501523468864543)
XLA Ops:
  7.2 0.7 all-gather.9.cloned.1.call-update
  8.0 0.7 all-gather.7.cloned.1.call-update
  8.7 1.3 dynamic-slice.1
  10.0 1.3 dynamic-slice
  12.6 0.8 copy.70
  13.3 2.3 reduce-window.6
  15.6 0.2 slice_reduce_fusion
  15.8 0.1 copy_bitcast_fusion
  15.8 0.2 slice_reduce_fusion.1
  16.1 0.1 fusion.63
  16.2 1.5 copy.74
  17.7 2.6 copy.75
  20.3 0.1 exponential_dynamic-update-slice_fusion
  20.4 2.4 all-reduce
  22.9 0.2 broadcast_select_fusion.1
  23.1 2.1 convolution_convert_fusion.1
  25.2 29.5 %all-gather.9.cloned.1.call-done = bf16[4096,512]{1,0:T(8,128)(2,1)} async-done(((bf16[256,512]{1,0:T(8,128)(2,1)}), bf16[4096,512]{1,0:T(8,128)(2,1)}) %all-gather.9.cloned.1.call-update) | async-done | bytes 4194320 | tf_op jit(solution)/shard_map/all_gather | solution.py:68
  54.7 82.9 %all-gather.7.cloned.1.call-done = bf16[1024,4096]{1,0:T(8,128)(2,1)} async-done(((bf16[1024,256]{1,0:T(8,128)(2,1)}), bf16[1024,4096]{1,0:T(8,128)(2,1)}) %all-gather.7.cloned.1.call-update) | async-done | bytes 8388624 | tf_op jit(solution)/shard_map/all_gather | solution.py:58
  137.6 11.3 %multiply_reduce_fusion.1 = (f32[1024]{0:T(1024)S(1)}, f32[1024]{0:T(1024)S(1)}, f32[1024,512]{0,1:T(8,128)}) fusion(bf16[1024,512]{0,1:T(8,128)(2,1)S(1)} %copy.74, bf16[1024,512]{0,1:T(8,128)(2,1)} %copy.75, f32[512]{0:T(512)S(1)} %copy-done.7, bf16[1024,4096]{1,0:T(8,128)(2,1)} %all-gather.7.cloned.1.call-done, ...), kind=kOutput, calls=%fused_computation.32 | convolution fusion | flops 4301256704 | bytes 16787456 | tf_op jit(solution)/shard_map/dot_general | solution.py:66
  148.8 8.7 %all-reduce.3 = (f32[1024]{0:T(1024)S(1)}, f32[1024]{0:T(1024)S(1)}) all-reduce(f32[1024]{0:T(1024)S(1)} %get-tuple-element.160, f32[1024]{0:T(1024)S(1)} %get-tuple-element.159), channel_id=1, replica_groups=mesh['seq_0'=8,'seq_1'=2,'head_0'=4,'head_1'=4] {'head_0'}, use_global_device_ids=true, to_apply=%region_6.0 | all-reduce | flops 2048 | bytes 16384 | tf_op jit(solution)/shard_map/psum | solution.py:18
  157.5 10.2 %all-reduce.2 = (f32[1024]{0:T(1024)S(1)}, f32[1024]{0:T(1024)S(1)}) all-reduce(f32[1024]{0:T(1024)S(1)} %get-tuple-element.175, f32[1024]{0:T(1024)S(1)} %get-tuple-element.176), channel_id=1, replica_groups=mesh['seq_0'=8,'seq_1'=2,'head_0'=4,'head_1'=4] {'head_1'}, use_global_device_ids=true, to_apply=%region_7.8 | all-reduce | flops 2048 | bytes 16384 | tf_op jit(solution)/shard_map/psum | solution.py:18
  167.8 4.7 %fusion.9 = (bf16[1024,512]{0,1:T(8,128)(2,1)}, bf16[1024,512]{0,1:T(8,128)(2,1)S(1)}) fusion(bf16[1024,512]{0,1:T(8,128)(2,1)S(1)} %copy.74, bf16[1024,512]{0,1:T(8,128)(2,1)} %copy.75, f32[1024]{0:T(1024)S(1)} %get-tuple-element.173, f32[1024]{0:T(1024)S(1)} %get-tuple-element.182, f32[1024,512]{0,1:T(8,128)} %get-tuple-element.195, f32[512]{0:T(512)S(1)} %copy-done.7, ...), kind=kLoop, calls=%fused_computation.20 | loop fusion | flops 11534336 | bytes 6305792 | tf_op jit(solution)/shard_map/convert_element_type | solution.py:81
  172.5 1.8 fusion.27
  174.2 0.1 broadcast_in_dim.27
  174.3 4.5 %while.17 = (s32[]{:T(128)}, f32[8,64,128]{2,1,0:T(8,128)S(1)}, f32[4,8,64,128]{3,2,1,0:T(8,128)S(1)}, f32[4,8,64,128]{3,2,0,1:T(8,128)}, f32[4,8]{1,0:T(4,128)S(1)}, /*index=5*/s32[]{:T(128)}, s32[]{:T(128)}, s32[]{:T(128)}) while((s32[]{:T(128)}, f32[8,64,128]{2,1,0:T(8,128)S(1)}, f32[4,8,64,128]{3,2,1,0:T(8,128)S(1)}, ...), condition=%wide.region_9.10_spmd.clone, body=%wide.region_8.9_spmd.clone.sunk | while | flops 262148 | bytes 1310944 | solution.py:135
  174.4 1.1 bitcast_add_fusion.4
  175.5 1.1 bitcast_add_fusion.4
  176.6 1.1 bitcast_add_fusion.4
  177.8 1.1 bitcast_add_fusion.4
  178.8 1.0 copy-done.4
  179.8 2.2 all-gather
  182.0 0.8 fusion.55
  182.8 0.2 reduce-scatter.2.cloned.1.call-start
  183.0 11.0 %fusion.2 = bf16[4096,512]{0,1:T(8,128)(2,1)} fusion(bf16[1024,4096]{1,0:T(8,128)(2,1)} %all-gather.7.cloned.1.call-done, f32[512]{0:T(512)S(1)} %copy-done.7, bf16[1024,512]{0,1:T(8,128)(2,1)} %copy-done.2, f32[1024]{0:T(1024)S(1)} %get-tuple-element.181, bf16[1024,512]{0,1:T(8,128)(2,1)} %copy.75), kind=kOutput, calls=%fused_computation.7 | convolution fusion | flops 4302307328 | bytes 14686208 | tf_op jit(solution)/shard_map/dot_general | solution.py:85
  194.2 0.7 copy-done.6
  194.9 17.7 %all-reduce.1 = f32[64]{0:T(128)S(1)} all-reduce(f32[64]{0:T(128)S(1)} %copy-done.10), channel_id=4, replica_groups=mesh['seq_0'=8,'seq_1'=2,'head_0'=4,'head_1'=4] {'seq_0'}, use_global_device_ids=true, to_apply=%add.1 | all-reduce | flops 64 | bytes 512
  212.6 0.1 fusion.64
  212.7 3.7 %convolution_convert_fusion.2 = bf16[8,1024,128]{2,0,1:T(8,128)(2,1)} fusion(bf16[1024,8,128]{2,1,0:T(8,128)(2,1)} %param.19, s32[8]{0:T(128)S(1)} %and_select_fusion), kind=kOutput, calls=%fused_computation.34 | convolution fusion | flops 17825856 | bytes 4194336 | tf_op jit(solution)/shard_map/tgn,hg->htn/dot_general | solution.py:104
  216.3 2.3 copy.86
  218.6 6.3 %fusion.3 = f32[8,4,256,64]{2,3,1,0:T(8,128)} fusion(f32[8,4,256]{2,1,0:T(4,128)S(1)} %copy.72, pred[256,256]{1,0:T(8,128)(4,1)S(1)} %iota_compare_fusion, bf16[8,4,256,128]{3,0,2,1:T(8,128)(2,1)} %bitcast.136, bf16[8,4,256,128]{3,0,2,1:T(8,128)(2,1)} %bitcast.130, bf16[8,8,4,8,256]{4,3,2,1,0:T(8,128)(2,1)} %bitcast.133), kind=kOutput, calls=%fused_computation.8 | convolution fusion | flops 815792128 | bytes 7438336 | tf_op jit(solution)/shard_map/hkts,hksp->hktp/dot_general | solution.py:123
  224.9 2.1 fusion.53
  227.0 0.1 copy-done.1
  227.2 3.3 %fusion.30 = bf16[8,4,8,8,256]{4,3,2,1,0:T(8,128)(2,1)S(1)} fusion(f32[8,4,256,64]{2,3,1,0:T(8,128)} %fusion.3, bf16[8,4,256,128]{3,0,2,1:T(8,128)(2,1)S(1)} %bitcast.131, f32[8]{0:T(128)S(1)} %copy-done.8, f32[8,4,256]{2,1,0:T(4,128)S(1)} %copy.83, f32[8,4,256]{2,1,0:T(4,128)S(1)} %copy.67, bf16[8,8,4,8,256]{4,3,2,1,0:T(8,128)(2,1)} %bitcast.134, ...), kind=kOutput, calls=%fused_computation.42 | convolution fusion | flops 138674176 | bytes 7667872 | tf_op jit(solution)/shard_map/hkpn,hktn->hktp/dot_general | solution.py:151
  230.5 0.1 copy.91
  230.6 1.3 copy.85
  231.9 53.7 %reduce-scatter.2.cloned.1.call-done = bf16[256,512]{0,1:T(8,128)(2,1)} async-done(((bf16[4096,512]{0,1:T(8,128)(2,1)}), bf16[256,512]{0,1:T(8,128)(2,1)}) %reduce-scatter.2.cloned.1.call-update) | async-done | bytes 262160 | tf_op jit(solution)/shard_map/reduce_scatter | solution.py:84
  285.6 1.0 convert_multiply_fusion.7
  286.6 1.0 copy.87
  (47 shorter events, 0.5 us)
Async XLA Ops:
  7.2 15.9 %copy-start = (bf16[1024,8,128]{2,1,0:T(8,128)(2,1)S(1)}, bf16[1024,8,128]{2,1,0:T(8,128)(2,1)}, u32[]{:S(2)}) copy-start(bf16[1024,8,128]{2,1,0:T(8,128)(2,1)} %param.20) | copy-start | bytes 6291460
  7.2 47.5 %all-gather.9.cloned.1.call-start = ((), (), s32[]{:S(2)}) async-start(), calls=%async_computation.2 | async-start | bytes 4456448 | tf_op jit(solution)/shard_map/all_gather | solution.py:68
  7.9 129.7 %all-gather.7.cloned.1.call-start = ((), (), s32[]{:S(2)}) async-start(), calls=%async_computation.1 | async-start | bytes 8912896 | tf_op jit(solution)/shard_map/all_gather | solution.py:58
  8.7 216.3 %all-gather.11.cloned.1.call-start = ((), (), s32[]{:S(2)}) async-start(), calls=%async_computation.3 | async-start | bytes 2359296 | tf_op jit(solution)/shard_map/all_gather | solution.py:33
  17.7 150.1 %copy-start.2 = (bf16[1024,512]{0,1:T(8,128)(2,1)}, bf16[1024,512]{0,1:T(8,128)(2,1)S(1)}, u32[]{:S(2)}) copy-start(bf16[1024,512]{0,1:T(8,128)(2,1)S(1)} %copy.74) | copy-start | bytes 3145732
  23.1 2.1 copy-start.9
  23.1 114.5 %copy-start.7 = (f32[512]{0:T(512)S(1)}, f32[512]{0:T(512)}, u32[]{:S(2)}) copy-start(f32[512]{0:T(512)} %param.16) | copy-start | bytes 6148
  167.8 4.7 %copy-start.5 = (bf16[8,1024,128]{2,0,1:T(8,128)(2,1)S(1)}, bf16[8,1024,128]{2,0,1:T(8,128)(2,1)}, u32[]{:S(2)}) copy-start(bf16[8,1024,128]{2,0,1:T(8,128)(2,1)} %convolution_convert_fusion.1) | copy-start | bytes 6291460
  172.5 1.8 copy-start.3
  178.8 1.0 copy-start.4
  182.8 102.8 %reduce-scatter.2.cloned.1.call-start = ((), (), s32[]{:S(2)}) async-start(), calls=%async_computation.4 | async-start | bytes 4456448 | tf_op jit(solution)/shard_map/reduce_scatter | solution.py:84
  194.0 0.8 copy-start.6
  194.1 0.8 copy-start.10
  224.9 2.1 copy-start.8
  224.9 2.2 copy-start.1
Sparse Core Ops, SparseCore 0:
  9.8 44.8 all-gather.8
  57.1 80.4 all-gather.6
  182.9 38.5 all-gather.10
  223.9 61.6 reduce-scatter.1
where the time goes:
time: 295 us; the launch traced here: 294 us
  waiting for transfers between devices  167 us (57%)
  blocking collectives  41.2 us (14%)
  matrix products  39.5 us (13%)
  other arithmetic  15.8 us (5%)
  between operations  15.3 us (5%)
  local copies, waits for them, and re-layouts  14.4 us (5%)
    all_gather x1, waiting for transfers between devices, on_device(): full_grad = lax.all_gather(grad_output, HEAD, axis=1, tiled=True)  82.9 us
    reduce_scatter x1, waiting for transfers between devices, on_device(): lax.psum_scatter(lax.dot_general(columns, normed, (((0,), (0,)), ((), ())...  53.7 us
    all_gather x1, waiting for transfers between devices, on_device(): lax.all_gather(out_weight, SEQ, axis=0, tiled=True)  29.5 us
    unnamed x2, blocking collectives  20.1 us
    psum x2, blocking collectives, over_axes(): x = lax.psum(x, axis)  18.9 us
    unnamed x32, local copies, waits for them, and re-layouts  13.2 us
    dot_general x1, matrix products, on_device(): jnp.dot(columns, lax.all_gather(out_weight, SEQ, axis=0, tiled=True), pre...  11.3 us
    dot_general x1, matrix products, on_device(): lax.dot_general(columns, normed, (((0,), (0,)), ((), ())), preferred_elem...  11 us
  transfers between devices with their start and end apart: 4, of which 3 were waited for; matrix products, arithmetic and copies ran while one was open for 15% of the time, Pallas kernels for 0%

commit v1 on v0

--- a/solution.py
+++ b/solution.py
@@ -15,7 +15,7 @@
 
 def over_axes(x, axes):
     for axis in axes:
-        x = lax.psum(x, axis)
+        x = jnp.sum(lax.all_gather(x, axis), axis=0)
     return x
 
 

time: 295 us -> 326 us (1.11)
  blocking collectives: 41.2 us -> 70.2 us
    all_gather x0 -> x4, blocking collectives: none -> 48.1 us  [over_axes(): x = jnp.sum(lax.all_gather(x, axis), axis=0)]
    psum x2 -> x0, blocking collectives: 18.9 us -> none  [over_axes(): x = lax.psum(x, axis)]
    unnamed x32 -> x48, local copies, waits for them, and re-layouts: 13.2 us -> 13.2 us
  transfers between devices with their start and end apart: 4 -> 4, of which waited for: 3 -> 3; matrix products, arithmetic and copies ran while one was open for 15% -> 13% of each run, Pallas kernels for 0% -> 0%
where the time goes in v1:
time: 326 us; the launch traced here: 325 us
  waiting for transfers between devices  169 us (52%)
  blocking collectives  70.2 us (22%)
  matrix products  39.5 us (12%)
  other arithmetic  16.3 us (5%)
  between operations  15.4 us (5%)
  local copies, waits for them, and re-layouts  14.5 us (4%)
    all_gather x1, waiting for transfers between devices, on_device(): full_grad = lax.all_gather(grad_output, HEAD, axis=1, tiled=True)  82.9 us
    reduce_scatter x1, waiting for transfers between devices, on_device(): lax.psum_scatter(lax.dot_general(columns, normed, (((0,), (0,)), ((), ())...  55.4 us
    all_gather x4, blocking collectives, over_axes(): x = jnp.sum(lax.all_gather(x, axis), axis=0)  48.1 us
    all_gather x1, waiting for transfers between devices, on_device(): lax.all_gather(out_weight, SEQ, axis=0, tiled=True)  29 us
    unnamed x2, blocking collectives  20 us
    unnamed x48, local copies, waits for them, and re-layouts  13.2 us
    dot_general x1, matrix products, on_device(): jnp.dot(columns, lax.all_gather(out_weight, SEQ, axis=0, tiled=True), pre...  11.3 us
    dot_general x1, matrix products, on_device(): lax.dot_general(columns, normed, (((0,), (0,)), ((), ())), preferred_elem...  11 us
  transfers between devices with their start and end apart: 4, of which 3 were waited for; matrix products, arithmetic and copies ran while one was open for 13% of the time, Pallas kernels for 0%

profile of v1, /device:TPU:2, one launch (start us, length us, event | category | flops | bytes accessed | tf_op | source)
XLA Modules:
  0.0 325.1 jit_solution(12308254657206856414)
XLA Ops:
  7.2 0.7 all-gather.13.cloned.1.call-update
  8.0 0.7 all-gather.11.cloned.1.call-update
  8.7 1.3 dynamic-slice.1
  10.0 1.3 dynamic-slice
  12.6 0.8 copy.91
  13.3 2.3 reduce-window.6
  15.6 0.2 slice_reduce_fusion
  15.8 0.2 slice_reduce_fusion.1
  16.1 0.1 fusion.63
  16.2 1.5 copy.95
  17.7 2.6 copy.96
  20.3 0.1 exponential_dynamic-update-slice_fusion
  20.4 2.4 all-reduce
  22.9 0.7 broadcast_select_fusion.1
  23.6 2.1 convolution_convert_fusion.1
  25.7 29.0 %all-gather.13.cloned.1.call-done = bf16[4096,512]{1,0:T(8,128)(2,1)} async-done(((bf16[256,512]{1,0:T(8,128)(2,1)}), bf16[4096,512]{1,0:T(8,128)(2,1)}) %all-gather.13.cloned.1.call-update) | async-done | bytes 4194320 | tf_op jit(solution)/shard_map/all_gather | solution.py:68
  54.7 82.9 %all-gather.11.cloned.1.call-done = bf16[1024,4096]{1,0:T(8,128)(2,1)} async-done(((bf16[1024,256]{1,0:T(8,128)(2,1)}), bf16[1024,4096]{1,0:T(8,128)(2,1)}) %all-gather.11.cloned.1.call-update) | async-done | bytes 8388624 | tf_op jit(solution)/shard_map/all_gather | solution.py:58
  137.6 11.3 %multiply_reduce_fusion.1 = (f32[1024]{0:T(1024)S(1)}, f32[1024]{0:T(1024)S(1)}, f32[1024,512]{0,1:T(8,128)}) fusion(bf16[1024,512]{0,1:T(8,128)(2,1)S(1)} %copy.95, bf16[1024,512]{0,1:T(8,128)(2,1)} %copy.96, f32[512]{0:T(512)S(1)} %copy-done.9, bf16[1024,4096]{1,0:T(8,128)(2,1)} %all-gather.11.cloned.1.call-done, ...), kind=kOutput, calls=%fused_computation.32 | convolution fusion | flops 4301256704 | bytes 16787456 | tf_op jit(solution)/shard_map/dot_general | solution.py:66
  148.8 12.0 %all-gather = f32[4096]{0:T(1024)S(1)} all-gather(f32[1024]{0:T(1024)S(1)} %get-tuple-element.167), channel_id=2, replica_groups=mesh['seq_0'=8,'seq_1'=2,'head_0'=4,'head_1'=4] {'head_0'}, dimensions={0}, use_global_device_ids=true | all-gather | bytes 20480 | tf_op jit(solution)/shard_map/all_gather | solution.py:18
  160.9 12.0 %all-gather.1 = f32[4096]{0:T(1024)S(1)} all-gather(f32[1024]{0:T(1024)S(1)} %reduce_sum.68), channel_id=3, replica_groups=mesh['seq_0'=8,'seq_1'=2,'head_0'=4,'head_1'=4] {'head_1'}, dimensions={0}, use_global_device_ids=true | all-gather | bytes 20480 | tf_op jit(solution)/shard_map/all_gather | solution.py:18
  173.0 12.0 %all-gather.2 = f32[4096]{0:T(1024)S(1)} all-gather(f32[1024]{0:T(1024)S(1)} %get-tuple-element.168), channel_id=4, replica_groups=mesh['seq_0'=8,'seq_1'=2,'head_0'=4,'head_1'=4] {'head_0'}, dimensions={0}, use_global_device_ids=true | all-gather | bytes 20480 | tf_op jit(solution)/shard_map/all_gather | solution.py:18
  185.0 12.0 %all-gather.3 = f32[4096]{0:T(1024)S(1)} all-gather(f32[1024]{0:T(1024)S(1)} %reduce_sum.71), channel_id=5, replica_groups=mesh['seq_0'=8,'seq_1'=2,'head_0'=4,'head_1'=4] {'head_1'}, dimensions={0}, use_global_device_ids=true | all-gather | bytes 20480 | tf_op jit(solution)/shard_map/all_gather | solution.py:18
  197.1 4.6 %fusion.9 = (bf16[1024,512]{0,1:T(8,128)(2,1)}, bf16[1024,512]{0,1:T(8,128)(2,1)S(1)}) fusion(bf16[1024,512]{0,1:T(8,128)(2,1)S(1)} %copy.95, bf16[1024,512]{0,1:T(8,128)(2,1)} %copy.96, f32[1024]{0:T(1024)S(1)} %reduce_sum.72, f32[1024]{0:T(1024)S(1)} %get-tuple-element.186, f32[1024,512]{0,1:T(8,128)} %get-tuple-element.199, f32[512]{0:T(512)} %param.16, ...), kind=kLoop, calls=%fused_computation.20 | loop fusion | flops 11534336 | bytes 6305792 | tf_op jit(solution)/shard_map/convert_element_type | solution.py:81
  201.7 1.8 fusion.27
  203.5 0.1 broadcast_in_dim.27
  203.6 4.5 %while.17 = (s32[]{:T(128)}, f32[8,64,128]{2,1,0:T(8,128)S(1)}, f32[4,8,64,128]{3,2,1,0:T(8,128)S(1)}, f32[4,8,64,128]{3,2,0,1:T(8,128)}, f32[4,8]{1,0:T(4,128)S(1)}, /*index=5*/s32[]{:T(128)}, s32[]{:T(128)}, s32[]{:T(128)}) while((s32[]{:T(128)}, f32[8,64,128]{2,1,0:T(8,128)S(1)}, f32[4,8,64,128]{3,2,1,0:T(8,128)S(1)}, ...), condition=%wide.region_9.10_spmd.clone, body=%wide.region_8.9_spmd.clone.sunk | while | flops 262148 | bytes 1310944 | solution.py:135
  203.7 1.1 bitcast_add_fusion.4
  204.8 1.1 bitcast_add_fusion.4
  205.9 1.1 bitcast_add_fusion.4
  207.1 1.1 bitcast_add_fusion.4
  208.1 1.0 copy-done.4
  209.1 2.2 all-gather.4
  211.3 0.8 fusion.55
  212.1 0.2 reduce-scatter.2.cloned.1.call-start
  212.4 11.0 %fusion.2 = bf16[4096,512]{0,1:T(8,128)(2,1)} fusion(bf16[1024,4096]{1,0:T(8,128)(2,1)} %all-gather.11.cloned.1.call-done, f32[512]{0:T(512)S(1)} %copy-done.10, bf16[1024,512]{0,1:T(8,128)(2,1)} %copy-done.2, f32[1024]{0:T(1024)S(1)} %get-tuple-element.185, bf16[1024,512]{0,1:T(8,128)(2,1)} %copy.96), kind=kOutput, calls=%fused_computation.7 | convolution fusion | flops 4302307328 | bytes 14686208 | tf_op jit(solution)/shard_map/dot_general | solution.py:85
  223.5 0.6 copy-done.6
  224.2 17.5 %all-reduce.1 = f32[64]{0:T(128)S(1)} all-reduce(f32[64]{0:T(128)S(1)} %copy-done.18), channel_id=8, replica_groups=mesh['seq_0'=8,'seq_1'=2,'head_0'=4,'head_1'=4] {'seq_0'}, use_global_device_ids=true, to_apply=%add.1 | all-reduce | flops 64 | bytes 512
  241.8 3.7 %convolution_convert_fusion.2 = bf16[8,1024,128]{2,0,1:T(8,128)(2,1)} fusion(bf16[1024,8,128]{2,1,0:T(8,128)(2,1)} %param.19, s32[8]{0:T(128)S(1)} %copy-done.12), kind=kOutput, calls=%fused_computation.34 | convolution fusion | flops 17825856 | bytes 4194336 | tf_op jit(solution)/shard_map/tgn,hg->htn/dot_general | solution.py:104
  245.5 2.3 copy.107
  247.8 6.4 %fusion.3 = f32[8,4,256,64]{2,3,1,0:T(8,128)} fusion(f32[8,4,256]{2,1,0:T(4,128)S(1)} %copy.93, pred[256,256]{1,0:T(8,128)(4,1)S(1)} %iota_compare_fusion, bf16[8,4,256,128]{3,0,2,1:T(8,128)(2,1)} %bitcast.136, bf16[8,4,256,128]{3,0,2,1:T(8,128)(2,1)} %bitcast.130, bf16[8,8,4,8,256]{4,3,2,1,0:T(8,128)(2,1)} %bitcast.133), kind=kOutput, calls=%fused_computation.8 | convolution fusion | flops 815792128 | bytes 7438336 | tf_op jit(solution)/shard_map/hkts,hksp->hktp/dot_general | solution.py:123
  254.1 2.1 fusion.53
  256.2 0.1 copy-done.1
  256.4 3.3 %fusion.30 = bf16[8,4,8,8,256]{4,3,2,1,0:T(8,128)(2,1)S(1)} fusion(f32[8,4,256,64]{2,3,1,0:T(8,128)} %fusion.3, bf16[8,4,256,128]{3,0,2,1:T(8,128)(2,1)S(1)} %bitcast.131, f32[8]{0:T(128)S(1)} %copy-done.16, f32[8,4,256]{2,1,0:T(4,128)S(1)} %copy.104, f32[8,4,256]{2,1,0:T(4,128)S(1)} %copy.88, bf16[8,8,4,8,256]{4,3,2,1,0:T(8,128)(2,1)} %bitcast.134, ...), kind=kOutput, calls=%fused_computation.42 | convolution fusion | flops 138674176 | bytes 7667872 | tf_op jit(solution)/shard_map/hkpn,hktn->hktp/dot_general | solution.py:151
  259.7 0.1 copy.112
  259.8 1.3 copy.106
  261.1 55.4 %reduce-scatter.2.cloned.1.call-done = bf16[256,512]{0,1:T(8,128)(2,1)} async-done(((bf16[4096,512]{0,1:T(8,128)(2,1)}), bf16[256,512]{0,1:T(8,128)(2,1)}) %reduce-scatter.2.cloned.1.call-update) | async-done | bytes 262160 | tf_op jit(solution)/shard_map/reduce_scatter | solution.py:84
  316.5 1.0 convert_multiply_fusion.7
  317.5 1.0 copy.108
  (73 shorter events, 0.8 us)
Async XLA Ops:
  7.2 16.4 %copy-start = (bf16[1024,8,128]{2,1,0:T(8,128)(2,1)S(1)}, bf16[1024,8,128]{2,1,0:T(8,128)(2,1)}, u32[]{:S(2)}) copy-start(bf16[1024,8,128]{2,1,0:T(8,128)(2,1)} %param.20) | copy-start | bytes 6291460
  7.2 47.5 %all-gather.13.cloned.1.call-start = ((), (), s32[]{:S(2)}) async-start(), calls=%async_computation.2 | async-start | bytes 4456448 | tf_op jit(solution)/shard_map/all_gather | solution.py:68
  7.9 129.7 %all-gather.11.cloned.1.call-start = ((), (), s32[]{:S(2)}) async-start(), calls=%async_computation.1 | async-start | bytes 8912896 | tf_op jit(solution)/shard_map/all_gather | solution.py:58
  8.7 245.5 %all-gather.15.cloned.1.call-start = ((), (), s32[]{:S(2)}) async-start(), calls=%async_computation.3 | async-start | bytes 2359296 | tf_op jit(solution)/shard_map/all_gather | solution.py:33
  16.1 4.3 %copy-start.13 = (f32[8]{0:T(128)}, f32[8]{0:T(128)S(1)}, u32[]{:S(2)}) copy-start(f32[8]{0:T(128)S(1)} %get-tuple-element.169) | copy-start | bytes 100
  17.7 179.4 %copy-start.2 = (bf16[1024,512]{0,1:T(8,128)(2,1)}, bf16[1024,512]{0,1:T(8,128)(2,1)S(1)}, u32[]{:S(2)}) copy-start(bf16[1024,512]{0,1:T(8,128)(2,1)S(1)} %copy.95) | copy-start | bytes 3145732
  22.9 2.8 copy-start.11
  23.6 2.1 copy-start.17
  23.6 114.0 %copy-start.9 = (f32[512]{0:T(512)S(1)}, f32[512]{0:T(512)}, u32[]{:S(2)}) copy-start(f32[512]{0:T(512)} %param.16) | copy-start | bytes 6148
  197.1 4.6 %copy-start.5 = (bf16[8,1024,128]{2,0,1:T(8,128)(2,1)S(1)}, bf16[8,1024,128]{2,0,1:T(8,128)(2,1)}, u32[]{:S(2)}) copy-start(bf16[8,1024,128]{2,0,1:T(8,128)(2,1)} %convolution_convert_fusion.1) | copy-start | bytes 6291460
  201.7 1.8 copy-start.3
  203.6 7.7 %copy-start.7 = (f32[8]{0:T(128)S(1)}, f32[8]{0:T(128)}, u32[]{:S(2)}) copy-start(f32[8]{0:T(128)} %get-tuple-element.188) | copy-start | bytes 100
  203.6 7.7 %copy-start.8 = (f32[8]{0:T(128)S(1)}, f32[8]{0:T(128)}, u32[]{:S(2)}) copy-start(f32[8]{0:T(128)} %get-tuple-element.190) | copy-start | bytes 100
  203.6 8.7 %copy-start.10 = (f32[512]{0:T(512)S(1)}, f32[512]{0:T(512)}, u32[]{:S(2)}) copy-start(f32[512]{0:T(512)} %param.16) | copy-start | bytes 6148
  208.1 1.0 copy-start.4
  212.1 104.4 %reduce-scatter.2.cloned.1.call-start = ((), (), s32[]{:S(2)}) async-start(), calls=%async_computation.4 | async-start | bytes 4456448 | tf_op jit(solution)/shard_map/reduce_scatter | solution.py:84
  223.4 0.8 copy-start.6
  223.4 0.8 copy-start.18
  223.4 18.4 %copy-start.14 = (f32[8]{0:T(128)S(1)}, f32[8]{0:T(128)}, u32[]{:S(2)}) copy-start(f32[8]{0:T(128)} %copy-done.13) | copy-start | bytes 100
  223.4 18.4 %copy-start.12 = (s32[8]{0:T(128)S(1)}, s32[8]{0:T(128)}, u32[]{:S(2)}) copy-start(s32[8]{0:T(128)} %copy-done.11) | copy-start | bytes 100
  247.8 6.4 %copy-start.15 = (f32[8]{0:T(128)S(1)}, f32[8]{0:T(128)}, u32[]{:S(2)}) copy-start(f32[8]{0:T(128)} %get-tuple-element.187) | copy-start | bytes 100
  254.1 2.1 copy-start.16
  254.1 2.2 copy-start.1
Sparse Core Ops, SparseCore 0:
  9.8 44.8 all-gather.12
  57.1 80.4 all-gather.10
  212.2 40.4 all-gather.14
  255.2 61.3 reduce-scatter.1
